TPU v7x, 512 devices: a whole 4x8x8 slice. The times are simulated.
512 devices in a mesh: dp: 32 (over z, y_hi), tensor: 16 (over x, y_lo, core).
Axes of the slice: x: 4, y: 8 (y_hi: 4, y_lo: 2; y = y_hi * 2 + y_lo), z: 8, core: 2. Of those that a mesh axis runs over, the one named last changes fastest.
Arguments:
- tokens_in: bfloat16 [4096, 4096], P(('dp', 'tensor')), may hold values from -6 to 6
- grad_out: bfloat16 [4096, 4096], P(('dp', 'tensor')), may hold values from -6 to 6
- gate_pre: bfloat16 [4096, 7168], P('dp', 'tensor'), may hold values from -6 to 6
- up_pre: bfloat16 [4096, 7168], P('dp', 'tensor'), may hold values from -6 to 6
- gate_weight: bfloat16 [4096, 7168], P('dp', 'tensor'), may hold values from -0.09375 to 0.09375
- up_weight: bfloat16 [4096, 7168], P('dp', 'tensor'), may hold values from -0.09375 to 0.09375
- down_weight: bfloat16 [7168, 4096], P('tensor', 'dp'), may hold values from -0.0625 to 0.0625
- norm_gain: float32 [4096], replicated, may hold values from 0.1 to 1.9
Outputs:
- input_grad: bfloat16 [4096, 4096], P(('dp', 'tensor'))
- gain_grad: float32 [4096], replicated
- down_grad: bfloat16 [7168, 4096], P('tensor', 'dp')
All inputs are finite; a program needn't handle non-finite values.
Results may differ from a plain program's by a relative error of at most 0.015.
Values may be sent and summed in bfloat16 or wider, within the bound.
A program may use at most 64 MiB of HBM per device.

v0:
```python
import jax
import jax.numpy as jnp
from jax import lax
from jax.sharding import Mesh
from jax.sharding import PartitionSpec as P

Z = "dp_0"
YH = "dp_1"
TENSOR = ("tensor_0", "tensor_1", "tensor_2")
DP = ("dp_0", "dp_1")
DP_TENSOR = ("dp_0", "dp_1", "tensor_0", "tensor_1", "tensor_2")


def nt(a, b):
    return lax.dot_general(a, b, (((1,), (1,)), ((), ())), preferred_element_type=jnp.float32)


def tn(a, b):
    return lax.dot_general(a, b, (((0,), (0,)), ((), ())), preferred_element_type=jnp.float32)


def swap(x, axis):
    return lax.all_to_all(x, axis, split_axis=0, concat_axis=0, tiled=True)


def per_device(
    tokens_in, grad_out, gate_pre, up_pre, gate_weight, up_weight, down_weight, norm_gain
):
    mine = swap(grad_out.reshape(8, 8, 4, 128).transpose(2, 0, 1, 3), YH)
    rows = lax.all_gather(mine.reshape(32, 1024), TENSOR, axis=0, tiled=True)
    rows = rows.reshape(16, 4, 8, 1024).transpose(1, 0, 2, 3).reshape(512, 1024)
    down = lax.all_gather(down_weight, Z, axis=1, tiled=True)
    gate_w = lax.all_gather(gate_weight, Z, axis=0, tiled=True)
    up_w = lax.all_gather(up_weight, Z, axis=0, tiled=True)
    gate = lax.all_gather(gate_pre, YH, axis=0, tiled=True).astype(jnp.float32)
    up = lax.all_gather(up_pre, YH, axis=0, tiled=True).astype(jnp.float32)
    sig = jax.nn.sigmoid(gate)
    silu = gate * sig
    act = (silu * up).astype(jnp.bfloat16)
    part = nt(rows, down).astype(jnp.bfloat16).reshape(4, 128, 448)
    grad_act = swap(part, YH).astype(jnp.float32).sum(axis=0).astype(jnp.bfloat16)
    grad_act = lax.all_gather(grad_act, YH, axis=0, tiled=True).astype(jnp.float32)
    grad_gate = (grad_act * up * sig * (1.0 + gate * (1.0 - sig))).astype(jnp.bfloat16)
    grad_up = (grad_act * silu).astype(jnp.bfloat16)
    norm = (nt(grad_gate, gate_w) + nt(grad_up, up_w)).astype(jnp.bfloat16)
    norm = norm.reshape(4, 16, 8, 1024).transpose(1, 0, 2, 3)
    norm = swap(norm, TENSOR).astype(jnp.float32).sum(axis=0)
    norm = swap(norm, YH).reshape(4, 8, 8, 128)
    grad_norm = norm.transpose(1, 2, 0, 3).reshape(8, 4096)
    total = tn(act, rows).astype(jnp.bfloat16).reshape(448, 8, 128).transpose(1, 0, 2)
    down_grad = swap(total, Z).astype(jnp.float32).sum(axis=0).astype(jnp.bfloat16)
    inputs = tokens_in.astype(jnp.float32)
    inv_rms = lax.rsqrt(jnp.mean(inputs * inputs, axis=1, keepdims=True) + 1e-05)
    normed = inputs * inv_rms
    gain_grad = lax.psum(jnp.sum(grad_norm * normed, axis=0), DP_TENSOR)
    scaled = grad_norm * norm_gain
    inner = jnp.mean(scaled * normed, axis=1, keepdims=True)
    input_grad = (grad_out.astype(jnp.float32) + inv_rms * (scaled - normed * inner)).astype(
        jnp.bfloat16
    )
    return (input_grad, gain_grad, down_grad)


def solution(mesh):
    finer = Mesh(
        mesh.devices.reshape(8, 4, 4, 2, 2), ("dp_0", "dp_1", "tensor_0", "tensor_1", "tensor_2")
    )
    return jax.shard_map(
        per_device,
        mesh=finer,
        in_specs=(
            P(DP_TENSOR, None),
            P(DP_TENSOR, None),
            P(DP, TENSOR),
            P(DP, TENSOR),
            P(DP, TENSOR),
            P(DP, TENSOR),
            P(TENSOR, DP),
            P(),
        ),
        out_specs=(P(DP_TENSOR, None), P(), P(TENSOR, DP)),
        check_vma=False,
    )
```

profile of v0, /device:TPU:1, one launch (start us, length us, event | category | flops | bytes accessed | tf_op | source)
XLA Modules:
  0.0 346.4 jit_solution(479711068150174751)
XLA Ops:
  7.2 0.0 all-gather.2.cloned.1.call-start
  7.2 0.9 copy.37
  8.1 14.3 %all_to_all.25 = bf16[4,8,8,128]{3,2,1,0:T(8,128)(2,1)S(1)} all-to-all(bf16[4,8,8,128]{3,2,1,0:T(8,128)(2,1)S(1)} %bitcast.51), channel_id=1, replica_groups=mesh['dp_0'=8,'dp_1'=4,'tensor_0'=4,'tensor_1'=2,'tensor_2'=2] {'dp_1'}, dimensions={0} | all-to-all | bytes 131072 | tf_op jit(solution)/shard_map/all_to_all | solution.py:23
  22.4 0.6 copy.36
  23.0 0.0 all-gather.2.cloned.1.call-update
  23.1 28.1 %all_gather.26 = bf16[1024,448]{0,1:T(8,128)(2,1)S(1)} all-gather(bf16[128,448]{0,1:T(8,128)(2,1)} %param.12), channel_id=1, replica_groups=mesh['dp_0'=8,'dp_1'=4,'tensor_0'=4,'tensor_1'=2,'tensor_2'=2] {'dp_0'}, dimensions={0}, use_global_device_ids=true | all-gather | bytes 1032192 | tf_op jit(solution)/shard_map/all_gather | solution.py:33
  51.2 22.6 %all_gather.22 = bf16[448,1024]{1,0:T(8,128)(2,1)S(1)} all-gather(bf16[448,128]{1,0:T(8,128)(2,1)} %param.14), channel_id=1, replica_groups=mesh['dp_0'=8,'dp_1'=4,'tensor_0'=4,'tensor_1'=2,'tensor_2'=2] {'dp_0'}, dimensions={1}, use_global_device_ids=true | all-gather | bytes 1032192 | tf_op jit(solution)/shard_map/all_gather | solution.py:32
  73.7 0.0 all-gather.2.cloned.1.call-done
  73.7 1.3 copy.17
  75.1 0.0 copy-start.5
  75.1 0.7 fusion.1
  75.7 0.0 copy-start.6
  75.8 0.8 copy.34
  76.6 3.5 all-to-all-start.1
  80.1 0.0 copy-done.5
  80.1 23.9 %all_gather.25 = bf16[512,448]{0,1:T(8,128)(2,1)S(1)} all-gather(bf16[128,448]{0,1:T(8,128)(2,1)S(1)} %copy-done.5), channel_id=1, replica_groups=mesh['dp_0'=8,'dp_1'=4,'tensor_0'=4,'tensor_1'=2,'tensor_2'=2] {'dp_1'}, dimensions={0}, use_global_device_ids=true | all-gather | bytes 573440 | tf_op jit(solution)/shard_map/all_gather | solution.py:35
  104.0 0.0 copy-done.6
  104.0 16.0 %all_gather.24 = bf16[512,448]{0,1:T(8,128)(2,1)S(1)} all-gather(bf16[128,448]{0,1:T(8,128)(2,1)S(1)} %copy-done.6), channel_id=1, replica_groups=mesh['dp_0'=8,'dp_1'=4,'tensor_0'=4,'tensor_1'=2,'tensor_2'=2] {'dp_1'}, dimensions={0}, use_global_device_ids=true | all-gather | bytes 573440 | tf_op jit(solution)/shard_map/all_gather | solution.py:36
  120.0 0.0 copy-start.2
  120.0 20.3 %all_gather.27 = bf16[1024,448]{0,1:T(8,128)(2,1)} all-gather(bf16[128,448]{0,1:T(8,128)(2,1)} %param.13), channel_id=1, replica_groups=mesh['dp_0'=8,'dp_1'=4,'tensor_0'=4,'tensor_1'=2,'tensor_2'=2] {'dp_0'}, dimensions={0}, use_global_device_ids=true | all-gather | bytes 1032192 | tf_op jit(solution)/shard_map/all_gather | solution.py:34
  140.4 0.0 all-to-all-done.1
  140.4 0.1 reduce_sum.61
  140.4 16.1 %all_gather.23 = bf16[512,448]{0,1:T(8,128)(2,1)S(1)} all-gather(bf16[128,448]{0,1:T(8,128)(2,1)S(1)} %reduce_sum.61), channel_id=1, replica_groups=mesh['dp_0'=8,'dp_1'=4,'tensor_0'=4,'tensor_1'=2,'tensor_2'=2] {'dp_1'}, dimensions={0}, use_global_device_ids=true | all-gather | bytes 573440 | tf_op jit(solution)/shard_map/all_gather | solution.py:42
  156.6 0.0 copy-start
  156.6 0.9 fusion.11
  157.5 0.0 copy-done.2
  157.5 0.2 copy-done
  157.8 0.8 add_convert_fusion
  158.6 0.0 copy-start.3
  158.6 1.1 copy.32
  159.7 25.8 %all-to-all-start.2 = ((bf16[16,4,8,1024]{3,2,1,0:T(8,128)(2,1)}), bf16[16,4,8,1024]{3,2,1,0:T(8,128)(2,1)S(1)}, u32[]{:S(2)}, u32[]{:S(2)}) async-start(bf16[16,4,8,1024]{3,2,1,0:T(8,128)(2,1)} %bitcast.36), calls=%async_computation.2 | async-start | bytes 2097152 | tf_op jit(solution)/shard_map/all_to_all | solution.py:23
  185.5 0.0 copy-done.3
  185.5 0.7 fusion
  186.2 0.0 copy-start.1
  186.2 1.1 copy.33
  187.4 13.8 %all-to-all-done.2 = bf16[16,4,8,1024]{3,2,1,0:T(8,128)(2,1)S(1)} async-done(((bf16[16,4,8,1024]{3,2,1,0:T(8,128)(2,1)}), bf16[16,4,8,1024]{3,2,1,0:T(8,128)(2,1)S(1)}, u32[]{:S(2)}, u32[]{:S(2)}) %all-to-all-start.2) | async-done | bytes 1048608 | tf_op jit(solution)/shard_map/all_to_all | solution.py:23
  201.1 4.5 %all-to-all-start.4 = ((bf16[8,448,128]{2,1,0:T(8,128)(2,1)}), bf16[8,448,128]{2,1,0:T(8,128)(2,1)S(1)}, u32[]{:S(2)}, u32[]{:S(2)}) async-start(bf16[8,448,128]{2,1,0:T(8,128)(2,1)} %bitcast.38), calls=%async_computation.4 | async-start | bytes 1835008 | tf_op jit(solution)/shard_map/all_to_all | solution.py:23
  205.6 0.0 copy-done.1
  205.6 0.0 copy-start.7
  205.6 0.0 copy-start.4
  205.6 0.1 fusion.25
  205.8 0.8 convert_reduce_fusion
  206.6 25.4 %all-to-all-done.4 = bf16[8,448,128]{2,1,0:T(8,128)(2,1)S(1)} async-done(((bf16[8,448,128]{2,1,0:T(8,128)(2,1)}), bf16[8,448,128]{2,1,0:T(8,128)(2,1)S(1)}, u32[]{:S(2)}, u32[]{:S(2)}) %all-to-all-start.4) | async-done | bytes 917536 | tf_op jit(solution)/shard_map/all_to_all | solution.py:23
  232.0 4.0 %all-to-all-start.3 = ((f32[4,8,1024]{2,1,0:T(8,128)}), f32[4,8,1024]{2,1,0:T(8,128)S(1)}, u32[]{:S(2)}, u32[]{:S(2)}) async-start(f32[4,8,1024]{2,1,0:T(8,128)} %convert_reduce_fusion), calls=%async_computation.3 | async-start | bytes 262144 | tf_op jit(solution)/shard_map/all_to_all | solution.py:23
  236.0 0.8 reduce_sum.65
  236.8 6.6 %all-to-all-done.3 = f32[4,8,1024]{2,1,0:T(8,128)S(1)} async-done(((f32[4,8,1024]{2,1,0:T(8,128)}), f32[4,8,1024]{2,1,0:T(8,128)S(1)}, u32[]{:S(2)}, u32[]{:S(2)}) %all-to-all-start.3) | async-done | bytes 131104 | tf_op jit(solution)/shard_map/all_to_all | solution.py:23
  243.4 0.1 copy.20
  243.5 0.1 reshape.53
  243.5 0.0 copy-done.7
  243.6 0.2 fusion.24
  243.8 95.1 %psum.7 = f32[4096]{0:T(1024)} all-reduce(f32[4096]{0:T(1024)S(1)} %get-tuple-element.3), channel_id=1, replica_groups=mesh['dp_0'=8,'dp_1'=4,'tensor_0'=4,'tensor_1'=2,'tensor_2'=2] {'dp_0','..., use_global_device_ids=true, to_apply=%region_5.0 | all-reduce | flops 4096 | bytes 32768 | tf_op jit(solution)/shard_map/psum | solution.py:55
  338.9 0.0 copy-done.4
  338.9 0.7 fusion.23
  (3 shorter events, 0.0 us)
Async XLA Ops:
  7.2 66.6 %all-gather.2.cloned.1.call-start = ((), (), s32[]{:S(2)}) async-start(), calls=%async_computation.5 | async-start | bytes 1114112 | tf_op jit(solution)/shard_map/all_gather | solution.py:30
  75.1 5.0 %copy-start.5 = (bf16[128,448]{0,1:T(8,128)(2,1)S(1)}, bf16[128,448]{0,1:T(8,128)(2,1)}, u32[]{:S(2)}) copy-start(bf16[128,448]{0,1:T(8,128)(2,1)} %param.10) | copy-start | bytes 344068
  75.7 28.2 %copy-start.6 = (bf16[128,448]{0,1:T(8,128)(2,1)S(1)}, bf16[128,448]{0,1:T(8,128)(2,1)}, u32[]{:S(2)}) copy-start(bf16[128,448]{0,1:T(8,128)(2,1)} %param.11) | copy-start | bytes 344068
  76.6 63.8 %all-to-all-start.1 = ((bf16[4,128,448]{1,2,0:T(8,128)(2,1)}), bf16[4,128,448]{1,2,0:T(8,128)(2,1)S(1)}, u32[]{:S(2)}, u32[]{:S(2)}) async-start(bf16[4,128,448]{1,2,0:T(8,128)(2,1)} %bitcast.39), calls=%async_computation.1 | async-start | bytes 917504 | tf_op jit(solution)/shard_map/all_to_all | solution.py:23
  120.0 37.5 %copy-start.2 = (bf16[512,448]{0,1:T(8,128)(2,1)}, bf16[512,448]{0,1:T(8,128)(2,1)S(1)}, u32[]{:S(2)}) copy-start(bf16[512,448]{0,1:T(8,128)(2,1)S(1)} %all_gather.24) | copy-start | bytes 1376260
  156.6 1.2 copy-start
  158.6 26.9 %copy-start.3 = (bf16[512,448]{0,1:T(8,128)(2,1)S(1)}, bf16[512,448]{0,1:T(8,128)(2,1)}, u32[]{:S(2)}) copy-start(bf16[512,448]{0,1:T(8,128)(2,1)} %copy-done.2) | copy-start | bytes 1376260
  159.7 41.5 %all-to-all-start.2 = ((bf16[16,4,8,1024]{3,2,1,0:T(8,128)(2,1)}), bf16[16,4,8,1024]{3,2,1,0:T(8,128)(2,1)S(1)}, u32[]{:S(2)}, u32[]{:S(2)}) async-start(bf16[16,4,8,1024]{3,2,1,0:T(8,128)(2,1)} %bitcast.36), calls=%async_computation.2 | async-start | bytes 2097152 | tf_op jit(solution)/shard_map/all_to_all | solution.py:23
  186.2 19.4 %copy-start.1 = (bf16[8,4096]{1,0:T(8,128)(2,1)S(1)}, bf16[8,4096]{1,0:T(8,128)(2,1)}, u32[]{:S(2)}) copy-start(bf16[8,4096]{1,0:T(8,128)(2,1)} %param.8) | copy-start | bytes 196612
  201.1 30.9 %all-to-all-start.4 = ((bf16[8,448,128]{2,1,0:T(8,128)(2,1)}), bf16[8,448,128]{2,1,0:T(8,128)(2,1)S(1)}, u32[]{:S(2)}, u32[]{:S(2)}) async-start(bf16[8,448,128]{2,1,0:T(8,128)(2,1)} %bitcast.38), calls=%async_computation.4 | async-start | bytes 1835008 | tf_op jit(solution)/shard_map/all_to_all | solution.py:23
  205.6 37.9 %copy-start.7 = (f32[4096]{0:T(1024)S(1)}, f32[4096]{0:T(1024)}, u32[]{:S(2)}) copy-start(f32[4096]{0:T(1024)} %param.15) | copy-start | bytes 49156
  205.6 133.2 %copy-start.4 = (bf16[8,4096]{1,0:T(8,128)(2,1)S(1)}, bf16[8,4096]{1,0:T(8,128)(2,1)}, u32[]{:S(2)}) copy-start(bf16[8,4096]{1,0:T(8,128)(2,1)} %param.9) | copy-start | bytes 196612
  232.0 11.4 %all-to-all-start.3 = ((f32[4,8,1024]{2,1,0:T(8,128)}), f32[4,8,1024]{2,1,0:T(8,128)S(1)}, u32[]{:S(2)}, u32[]{:S(2)}) async-start(f32[4,8,1024]{2,1,0:T(8,128)} %convert_reduce_fusion), calls=%async_computation.3 | async-start | bytes 262144 | tf_op jit(solution)/shard_map/all_to_all | solution.py:23
Sparse Core Ops, SparseCore 0:
  23.2 39.1 all-gather.1
where the time goes:
time: 347 us; the launch traced here: 346 us
  blocking collectives  236 us (68%)
  waiting for transfers between devices  45.7 us (13%)
  starting transfers between devices  37.8 us (11%)
  between operations  14.2 us (4%)
  local copies, waits for them, and re-layouts  6.3 us (2%)
    psum x1, blocking collectives, per_device(): gain_grad = lax.psum(jnp.sum(grad_norm * normed, axis=0), DP_TENSOR)  95.1 us
    all_to_all x4, waiting for transfers between devices, swap(): return lax.all_to_all(x, axis, split_axis=0, concat_axis=0, tiled=True)  45.7 us
    all_to_all x4, starting transfers between devices, swap(): return lax.all_to_all(x, axis, split_axis=0, concat_axis=0, tiled=True)  37.8 us
    all_gather x1, blocking collectives, per_device(): gate_w = lax.all_gather(gate_weight, Z, axis=0, tiled=True)  28.1 us
    all_gather x1, blocking collectives, per_device(): gate = lax.all_gather(gate_pre, YH, axis=0, tiled=True).astype(jnp.float32)  23.9 us
    all_gather x1, blocking collectives, per_device(): down = lax.all_gather(down_weight, Z, axis=1, tiled=True)  22.6 us
    all_gather x1, blocking collectives, per_device(): up_w = lax.all_gather(up_weight, Z, axis=0, tiled=True)  20.3 us
    all_gather x1, blocking collectives, per_device(): lax.all_gather(grad_act, YH, axis=0, tiled=True).astype(jnp.float32)  16.1 us
  transfers between devices with their start and end apart: 5, of which 3 were waited for; matrix products, arithmetic and copies ran while one was open for 1% of the time, Pallas kernels for 0%

commit v1 on v0

--- a/solution.py
+++ b/solution.py
@@ -31,7 +31,9 @@
     rows = rows.reshape(16, 4, 8, 1024).transpose(1, 0, 2, 3).reshape(512, 1024)
     down = lax.all_gather(down_weight, Z, axis=1, tiled=True)
     gate_w = lax.all_gather(gate_weight, Z, axis=0, tiled=True)
-    up_w = lax.all_gather(up_weight, Z, axis=0, tiled=True)
+    up_w = jnp.concatenate(
+        lax.all_to_all(jnp.stack([up_weight] * lax.axis_size(Z)), Z, 0, 0), axis=0
+    )
     gate = lax.all_gather(gate_pre, YH, axis=0, tiled=True).astype(jnp.float32)
     up = lax.all_gather(up_pre, YH, axis=0, tiled=True).astype(jnp.float32)
     sig = jax.nn.sigmoid(gate)

time: 347 us -> 351 us (1.012)
  waiting for transfers between devices: 45.7 us -> 57 us
  starting transfers between devices: 37.8 us -> 28.4 us
  matrix products: 3.15 us -> 7.42 us
    all_gather x1 -> x0, blocking collectives: 20.3 us -> none  [per_device(): up_w = lax.all_gather(up_weight, Z, axis=0, tiled=True)]
    all_to_all x1 -> x2, blocking collectives: 14.3 us -> 33.9 us  [swap(): return lax.all_to_all(x, axis, split_axis=0, concat_axis=0, tiled=True)]
    all_to_all x4 -> x3, starting transfers between devices: 37.8 us -> 21.9 us  [swap(): return lax.all_to_all(x, axis, split_axis=0, concat_axis=0, tiled=True)]
    all_gather x1, waiting for transfers between devices: 0.01 us -> 11.2 us  [per_device(): rows = lax.all_gather(mine.reshape(32, 1024), TENSOR, axis=0, tiled=True)]
    all_to_all x0 -> x1, starting transfers between devices: none -> 6.51 us  [per_device(): lax.all_to_all(jnp.stack([up_weight] * lax.axis_size(Z)), Z, 0, 0)]
    all_gather x1, blocking collectives: 22.6 us -> 28.1 us  [per_device(): down = lax.all_gather(down_weight, Z, axis=1, tiled=True)]
    all_gather x1, blocking collectives: 28.1 us -> 23 us  [per_device(): gate_w = lax.all_gather(gate_weight, Z, axis=0, tiled=True)]
    dot_general x3, matrix products: 2.43 us -> 6.69 us  [nt(): lax.dot_general(a, b, (((1,), (1,)), ((), ())), preferred_element_type=jn...]
  transfers between devices with their start and end apart: 5 -> 5, of which waited for: 3 -> 4; matrix products, arithmetic and copies ran while one was open for 1% -> 2% of each run, Pallas kernels for 0% -> 0%
where the time goes in v1:
time: 351 us; the launch traced here: 350 us
  blocking collectives  233 us (66%)
  waiting for transfers between devices  57 us (16%)
  starting transfers between devices  28.4 us (8%)
  between operations  14.2 us (4%)
  matrix products  7.42 us (2%)
  local copies, waits for them, and re-layouts  7.14 us (2%)
    psum x1, blocking collectives, per_device(): gain_grad = lax.psum(jnp.sum(grad_norm * normed, axis=0), DP_TENSOR)  95.1 us
    all_to_all x3, waiting for transfers between devices, swap(): return lax.all_to_all(x, axis, split_axis=0, concat_axis=0, tiled=True)  45.8 us
    all_to_all x2, blocking collectives, swap(): return lax.all_to_all(x, axis, split_axis=0, concat_axis=0, tiled=True)  33.9 us
    all_gather x1, blocking collectives, per_device(): down = lax.all_gather(down_weight, Z, axis=1, tiled=True)  28.1 us
    all_gather x1, blocking collectives, per_device(): gate_w = lax.all_gather(gate_weight, Z, axis=0, tiled=True)  23 us
    all_to_all x3, starting transfers between devices, swap(): return lax.all_to_all(x, axis, split_axis=0, concat_axis=0, tiled=True)  21.9 us
    all_gather x1, blocking collectives, per_device(): gate = lax.all_gather(gate_pre, YH, axis=0, tiled=True).astype(jnp.float32)  20.2 us
    all_gather x1, blocking collectives, per_device(): up = lax.all_gather(up_pre, YH, axis=0, tiled=True).astype(jnp.float32)  16.6 us
  transfers between devices with their start and end apart: 5, of which 4 were waited for; matrix products, arithmetic and copies ran while one was open for 2% of the time, Pallas kernels for 0%

profile of v1, /device:TPU:1, one launch (start us, length us, event | category | flops | bytes accessed | tf_op | source)
XLA Modules:
  0.0 350.1 jit_solution(10894852090322145741)
XLA Ops:
  7.2 0.0 all-gather.2.cloned.1.call-start
  7.2 0.9 copy.52
  8.1 14.3 %all_to_all.30 = bf16[4,8,8,128]{3,2,1,0:T(8,128)(2,1)S(1)} all-to-all(bf16[4,8,8,128]{3,2,1,0:T(8,128)(2,1)S(1)} %bitcast.58), channel_id=1, replica_groups=mesh['dp_0'=8,'dp_1'=4,'tensor_0'=4,'tensor_1'=2,'tensor_2'=2] {'dp_1'}, dimensions={0} | all-to-all | bytes 131072 | tf_op jit(solution)/shard_map/all_to_all | solution.py:23
  22.4 0.6 copy.51
  23.0 0.0 all-gather.2.cloned.1.call-update
  23.1 28.1 %all_gather.19 = bf16[448,1024]{1,0:T(8,128)(2,1)S(1)} all-gather(bf16[448,128]{1,0:T(8,128)(2,1)} %param.14), channel_id=1, replica_groups=mesh['dp_0'=8,'dp_1'=4,'tensor_0'=4,'tensor_1'=2,'tensor_2'=2] {'dp_0'}, dimensions={1}, use_global_device_ids=true | all-gather | bytes 1032192 | tf_op jit(solution)/shard_map/all_gather | solution.py:32
  51.2 11.2 %all-gather.2.cloned.1.call-done = bf16[512,1024]{1,0:T(8,128)(2,1)} async-done(((bf16[32,1024]{1,0:T(8,128)(2,1)}), bf16[512,1024]{1,0:T(8,128)(2,1)}) %all-gather.2.cloned.1.call-update) | async-done | bytes 1048592 | tf_op jit(solution)/shard_map/all_gather | solution.py:30
  62.4 1.3 copy.26
  63.7 0.0 copy-start.6
  63.7 0.7 fusion.1
  64.4 0.1 copy.49
  64.5 0.0 copy-start.7
  64.5 0.0 copy-start.8
  64.5 19.6 %all_to_all.31 = bf16[4,128,448]{1,2,0:T(8,128)(2,1)S(1)} all-to-all(bf16[4,128,448]{1,2,0:T(8,128)(2,1)S(1)} %bitcast.50), channel_id=1, replica_groups=mesh['dp_0'=8,'dp_1'=4,'tensor_0'=4,'tensor_1'=2,'tensor_2'=2] {'dp_1'}, dimensions={0} | all-to-all | bytes 917504 | tf_op jit(solution)/shard_map/all_to_all | solution.py:23
  84.1 0.0 copy-done.6
  84.1 0.0 copy-start.9
  84.1 1.0 stack.2
  85.1 6.5 %all-to-all-start.2 = ((bf16[8,128,448]{1,2,0:T(8,128)(2,1)}), bf16[8,128,448]{1,2,0:T(8,128)(2,1)S(1)}, u32[]{:S(2)}, u32[]{:S(2)}) async-start(bf16[8,128,448]{1,2,0:T(8,128)(2,1)} %stack.2), calls=%async_computation.2 | async-start | bytes 1835008 | tf_op jit(solution)/shard_map/all_to_all | solution.py:35
  91.6 0.0 copy-done.7
  91.7 20.2 %all_gather.22 = bf16[512,448]{0,1:T(8,128)(2,1)} all-gather(bf16[128,448]{0,1:T(8,128)(2,1)S(1)} %copy-done.7), channel_id=1, replica_groups=mesh['dp_0'=8,'dp_1'=4,'tensor_0'=4,'tensor_1'=2,'tensor_2'=2] {'dp_1'}, dimensions={0}, use_global_device_ids=true | all-gather | bytes 573440 | tf_op jit(solution)/shard_map/all_gather | solution.py:37
  111.9 0.0 copy-done.8
  111.9 16.6 %all_gather.21 = bf16[512,448]{0,1:T(8,128)(2,1)} all-gather(bf16[128,448]{0,1:T(8,128)(2,1)S(1)} %copy-done.8), channel_id=1, replica_groups=mesh['dp_0'=8,'dp_1'=4,'tensor_0'=4,'tensor_1'=2,'tensor_2'=2] {'dp_1'}, dimensions={0}, use_global_device_ids=true | all-gather | bytes 573440 | tf_op jit(solution)/shard_map/all_gather | solution.py:38
  128.5 0.0 copy-done.9
  128.5 23.0 %all_gather.23 = bf16[1024,448]{0,1:T(8,128)(2,1)S(1)} all-gather(bf16[128,448]{0,1:T(8,128)(2,1)S(1)} %copy-done.9), channel_id=1, replica_groups=mesh['dp_0'=8,'dp_1'=4,'tensor_0'=4,'tensor_1'=2,'tensor_2'=2] {'dp_0'}, dimensions={0}, use_global_device_ids=true | all-gather | bytes 1032192 | tf_op jit(solution)/shard_map/all_gather | solution.py:33
  151.5 0.1 reduce_sum.61
  151.6 16.2 %all_gather.20 = bf16[512,448]{0,1:T(8,128)(2,1)S(1)} all-gather(bf16[128,448]{0,1:T(8,128)(2,1)S(1)} %reduce_sum.61), channel_id=1, replica_groups=mesh['dp_0'=8,'dp_1'=4,'tensor_0'=4,'tensor_1'=2,'tensor_2'=2] {'dp_1'}, dimensions={0}, use_global_device_ids=true | all-gather | bytes 573440 | tf_op jit(solution)/shard_map/all_gather | solution.py:44
  167.8 0.0 copy-start.4
  167.8 0.8 copy-done.4
  168.6 0.0 copy-start.1
  168.6 3.5 fusion.13
  172.0 0.0 all-to-all-done.2
  172.0 0.0 copy-done.1
  172.0 2.5 add_convert_fusion
  174.6 0.0 copy-start.2
  174.6 0.0 copy-start.3
  174.6 1.1 copy.47
  175.7 14.0 %all-to-all-start.3 = ((bf16[16,4,8,1024]{3,2,1,0:T(8,128)(2,1)}), bf16[16,4,8,1024]{3,2,1,0:T(8,128)(2,1)S(1)}, u32[]{:S(2)}, u32[]{:S(2)}) async-start(bf16[16,4,8,1024]{3,2,1,0:T(8,128)(2,1)} %bitcast.42), calls=%async_computation.3 | async-start | bytes 2097152 | tf_op jit(solution)/shard_map/all_to_all | solution.py:23
  189.7 0.0 copy-done.2
  189.7 0.0 copy-done.3
  189.7 0.7 fusion
  190.5 0.0 copy-start
  190.5 1.2 copy.48
  191.6 13.8 %all-to-all-done.3 = bf16[16,4,8,1024]{3,2,1,0:T(8,128)(2,1)S(1)} async-done(((bf16[16,4,8,1024]{3,2,1,0:T(8,128)(2,1)}), bf16[16,4,8,1024]{3,2,1,0:T(8,128)(2,1)S(1)}, u32[]{:S(2)}, u32[]{:S(2)}) %all-to-all-start.3) | async-done | bytes 1048608 | tf_op jit(solution)/shard_map/all_to_all | solution.py:23
  205.5 4.2 %all-to-all-start.5 = ((bf16[8,448,128]{2,1,0:T(8,128)(2,1)}), bf16[8,448,128]{2,1,0:T(8,128)(2,1)S(1)}, u32[]{:S(2)}, u32[]{:S(2)}) async-start(bf16[8,448,128]{2,1,0:T(8,128)(2,1)} %bitcast.44), calls=%async_computation.5 | async-start | bytes 1835008 | tf_op jit(solution)/shard_map/all_to_all | solution.py:23
  209.6 0.0 copy-done
  209.6 0.0 copy-start.10
  209.6 0.0 copy-start.5
  209.7 0.1 fusion.27
  209.8 0.8 convert_reduce_fusion
  210.6 25.4 %all-to-all-done.5 = bf16[8,448,128]{2,1,0:T(8,128)(2,1)S(1)} async-done(((bf16[8,448,128]{2,1,0:T(8,128)(2,1)}), bf16[8,448,128]{2,1,0:T(8,128)(2,1)S(1)}, u32[]{:S(2)}, u32[]{:S(2)}) %all-to-all-start.5) | async-done | bytes 917536 | tf_op jit(solution)/shard_map/all_to_all | solution.py:23
  236.0 3.7 %all-to-all-start.4 = ((f32[4,8,1024]{2,1,0:T(8,128)}), f32[4,8,1024]{2,1,0:T(8,128)S(1)}, u32[]{:S(2)}, u32[]{:S(2)}) async-start(f32[4,8,1024]{2,1,0:T(8,128)} %convert_reduce_fusion), calls=%async_computation.4 | async-start | bytes 262144 | tf_op jit(solution)/shard_map/all_to_all | solution.py:23
  239.7 0.8 reduce_sum.65
  240.5 6.6 %all-to-all-done.4 = f32[4,8,1024]{2,1,0:T(8,128)S(1)} async-done(((f32[4,8,1024]{2,1,0:T(8,128)}), f32[4,8,1024]{2,1,0:T(8,128)S(1)}, u32[]{:S(2)}, u32[]{:S(2)}) %all-to-all-start.4) | async-done | bytes 131104 | tf_op jit(solution)/shard_map/all_to_all | solution.py:23
  247.0 0.1 copy.30
  247.1 0.1 reshape.59
  247.2 0.0 copy-done.10
  247.2 0.2 fusion.26
  247.4 95.1 %psum.7 = f32[4096]{0:T(1024)} all-reduce(f32[4096]{0:T(1024)S(1)} %get-tuple-element.3), channel_id=1, replica_groups=mesh['dp_0'=8,'dp_1'=4,'tensor_0'=4,'tensor_1'=2,'tensor_2'=2] {'dp_0','..., use_global_device_ids=true, to_apply=%region_5.0 | all-reduce | flops 4096 | bytes 32768 | tf_op jit(solution)/shard_map/psum | solution.py:57
  342.5 0.0 copy-done.5
  342.5 0.7 fusion.25
  (3 shorter events, 0.0 us)
Async XLA Ops:
  7.2 55.2 %all-gather.2.cloned.1.call-start = ((), (), s32[]{:S(2)}) async-start(), calls=%async_computation.6 | async-start | bytes 1114112 | tf_op jit(solution)/shard_map/all_gather | solution.py:30
  63.7 20.4 %copy-start.6 = (bf16[128,448]{0,1:T(8,128)(2,1)S(1)}, bf16[128,448]{0,1:T(8,128)(2,1)}, u32[]{:S(2)}) copy-start(bf16[128,448]{0,1:T(8,128)(2,1)} %param.13) | copy-start | bytes 344068
  64.5 27.2 %copy-start.7 = (bf16[128,448]{0,1:T(8,128)(2,1)S(1)}, bf16[128,448]{0,1:T(8,128)(2,1)}, u32[]{:S(2)}) copy-start(bf16[128,448]{0,1:T(8,128)(2,1)} %param.10) | copy-start | bytes 344068
  64.5 47.4 %copy-start.8 = (bf16[128,448]{0,1:T(8,128)(2,1)S(1)}, bf16[128,448]{0,1:T(8,128)(2,1)}, u32[]{:S(2)}) copy-start(bf16[128,448]{0,1:T(8,128)(2,1)} %param.11) | copy-start | bytes 344068
  84.1 44.4 %copy-start.9 = (bf16[128,448]{0,1:T(8,128)(2,1)S(1)}, bf16[128,448]{0,1:T(8,128)(2,1)}, u32[]{:S(2)}) copy-start(bf16[128,448]{0,1:T(8,128)(2,1)} %param.12) | copy-start | bytes 344068
  85.1 86.9 %all-to-all-start.2 = ((bf16[8,128,448]{1,2,0:T(8,128)(2,1)}), bf16[8,128,448]{1,2,0:T(8,128)(2,1)S(1)}, u32[]{:S(2)}, u32[]{:S(2)}) async-start(bf16[8,128,448]{1,2,0:T(8,128)(2,1)} %stack.2), calls=%async_computation.2 | async-start | bytes 1835008 | tf_op jit(solution)/shard_map/all_to_all | solution.py:35
  167.8 0.8 copy-start.4
  168.6 3.5 copy-start.1
  174.6 15.1 %copy-start.2 = (bf16[512,448]{0,1:T(8,128)(2,1)S(1)}, bf16[512,448]{0,1:T(8,128)(2,1)}, u32[]{:S(2)}) copy-start(bf16[512,448]{0,1:T(8,128)(2,1)} %all_gather.22) | copy-start | bytes 1376260
  174.6 15.1 %copy-start.3 = (bf16[512,448]{0,1:T(8,128)(2,1)S(1)}, bf16[512,448]{0,1:T(8,128)(2,1)}, u32[]{:S(2)}) copy-start(bf16[512,448]{0,1:T(8,128)(2,1)} %all_gather.21) | copy-start | bytes 1376260
  175.7 29.8 %all-to-all-start.3 = ((bf16[16,4,8,1024]{3,2,1,0:T(8,128)(2,1)}), bf16[16,4,8,1024]{3,2,1,0:T(8,128)(2,1)S(1)}, u32[]{:S(2)}, u32[]{:S(2)}) async-start(bf16[16,4,8,1024]{3,2,1,0:T(8,128)(2,1)} %bitcast.42), calls=%async_computation.3 | async-start | bytes 2097152 | tf_op jit(solution)/shard_map/all_to_all | solution.py:23
  190.5 19.2 %copy-start = (bf16[8,4096]{1,0:T(8,128)(2,1)S(1)}, bf16[8,4096]{1,0:T(8,128)(2,1)}, u32[]{:S(2)}) copy-start(bf16[8,4096]{1,0:T(8,128)(2,1)} %param.8) | copy-start | bytes 196612
  205.5 30.5 %all-to-all-start.5 = ((bf16[8,448,128]{2,1,0:T(8,128)(2,1)}), bf16[8,448,128]{2,1,0:T(8,128)(2,1)S(1)}, u32[]{:S(2)}, u32[]{:S(2)}) async-start(bf16[8,448,128]{2,1,0:T(8,128)(2,1)} %bitcast.44), calls=%async_computation.5 | async-start | bytes 1835008 | tf_op jit(solution)/shard_map/all_to_all | solution.py:23
  209.6 37.6 %copy-start.10 = (f32[4096]{0:T(1024)S(1)}, f32[4096]{0:T(1024)}, u32[]{:S(2)}) copy-start(f32[4096]{0:T(1024)} %param.15) | copy-start | bytes 49156
  209.6 132.9 %copy-start.5 = (bf16[8,4096]{1,0:T(8,128)(2,1)S(1)}, bf16[8,4096]{1,0:T(8,128)(2,1)}, u32[]{:S(2)}) copy-start(bf16[8,4096]{1,0:T(8,128)(2,1)} %param.9) | copy-start | bytes 196612
  236.0 11.0 %all-to-all-start.4 = ((f32[4,8,1024]{2,1,0:T(8,128)}), f32[4,8,1024]{2,1,0:T(8,128)S(1)}, u32[]{:S(2)}, u32[]{:S(2)}) async-start(f32[4,8,1024]{2,1,0:T(8,128)} %convert_reduce_fusion), calls=%async_computation.4 | async-start | bytes 262144 | tf_op jit(solution)/shard_map/all_to_all | solution.py:23
Sparse Core Ops, SparseCore 0:
  23.2 39.1 all-gather.1
